TPU v7x, 32 devices: a whole 2x2x4 slice. The times are simulated.
32 devices in a mesh: term: 16 (over z, x, core), sector: 2 (over y).
Axes of the slice: x: 2, y: 2, z: 4, core: 2. Of those that a mesh axis runs over, the one named last changes fastest.
Arguments:
- wavefunction: bfloat16 [4, 512, 512], P('sector'), may hold values from -6 to 6
- left_operators: bfloat16 [256, 512, 512], P(('term', 'sector')), may hold values from -0.25 to 0.25
- right_operators: bfloat16 [256, 512, 512], P(('term', 'sector')), may hold values from -0.25 to 0.25
- source_sector: int32 [256], P(('term', 'sector')), may hold values from 0 to 3
- target_sector: int32 [256], P(('term', 'sector')), may hold values from 0 to 3
- live_terms: int32 [32], P(('term', 'sector')), may hold values from 1 to 8, as said below
- sector_rows: int32 [4], replicated, may hold values from 1 to 512, as said below
Outputs:
- sigma_blocks: float32 [4, 512, 512], P('sector', 'term')
Inputs may be any that keep to these rules, and one draw needn't show every extreme that they name: Term group g = term index * 2 + sector index holds the term slots g * 8 to (g + 1) * 8 - 1; its live slots are the first live_terms[g]; some group has exactly 8. `sector_rows`: some sector uses exactly 512 rows.
All inputs are finite; a program needn't handle non-finite values.
Results may differ from a plain program's by a relative error of at most 0.0029.
Values may be sent and summed in bfloat16 or wider, within the bound.
A program may use at most 128 MiB of HBM per device.

v0:
```python
import jax
import jax.numpy as jnp
from jax import lax
from jax.sharding import PartitionSpec as P


def local(
    wavefunction,
    left_operators,
    right_operators,
    source_sector,
    target_sector,
    live_terms,
    sector_rows,
):
    whole_wave = lax.all_gather(wavefunction, "sector", axis=0, tiled=True)
    sector_count = whole_wave.shape[0]
    row_count = whole_wave.shape[1]
    col_count = whole_wave.shape[2]
    slot_count = left_operators.shape[0]
    row_ids = lax.iota(jnp.int32, row_count)
    live_mask = lax.iota(jnp.int32, slot_count) < live_terms[0]

    def term_product(slot):
        source_index = source_sector[slot]
        source = lax.dynamic_index_in_dim(whole_wave, source_index, 0, keepdims=False)
        keep_rows = (row_ids < sector_rows[source_index])[:, None]
        source = jnp.where(keep_rows, source, jnp.zeros_like(source))
        left_half = jnp.dot(
            left_operators[slot], source, preferred_element_type=jnp.float32
        ).astype(jnp.bfloat16)
        return lax.dot_general(
            left_half,
            right_operators[slot],
            (((1,), (1,)), ((), ())),
            preferred_element_type=jnp.float32,
        )

    partial_value = jnp.zeros((sector_count, row_count, col_count), jnp.float32)

    def apply_term(slot, partial_value):

        def contribute(partial_value):
            target_index = target_sector[slot]
            current = lax.dynamic_index_in_dim(partial_value, target_index, 0, keepdims=True)
            return lax.dynamic_update_index_in_dim(
                partial_value, current + term_product(slot)[None], target_index, 0
            )

        return lax.cond(live_mask[slot], contribute, lambda kept: kept, partial_value)

    partial_value = lax.fori_loop(0, slot_count, apply_term, partial_value)
    shares = lax.psum_scatter(partial_value, "term", scatter_dimension=1, tiled=True)
    owned = lax.psum_scatter(shares, "sector", scatter_dimension=0, tiled=True)
    owned_sectors = owned.shape[0]
    owned_rows = owned.shape[1]
    sector_ids = lax.axis_index("sector") * owned_sectors + lax.iota(jnp.int32, owned_sectors)
    global_rows = lax.axis_index("term") * owned_rows + lax.iota(jnp.int32, owned_rows)
    limits = sector_rows[sector_ids]
    used = global_rows[None, :, None] < limits[:, None, None]
    return jnp.where(used, owned, jnp.zeros_like(owned))


def solution(mesh):
    in_specs = (
        P("sector", None, None),
        P(("term", "sector"), None, None),
        P(("term", "sector"), None, None),
        P(("term", "sector")),
        P(("term", "sector")),
        P(("term", "sector")),
        P(),
    )
    out_specs = P("sector", "term", None)
    return jax.shard_map(local, mesh=mesh, in_specs=in_specs, out_specs=out_specs, check_vma=False)
```

profile of v0, /device:TPU:0, one launch (start us, length us, event | category | flops | bytes accessed | tf_op | source)
XLA Modules:
  0.0 229.0 jit_solution(8701649357026881521)
XLA Ops:
  6.5 0.7 all-gather.2.cloned.1.call-update
  7.3 0.0 reduce-scatter.3.cloned.1.call-start
  8.0 36.8 %all-gather.2.cloned.1.call-done = bf16[4,512,512]{2,1,0:T(8,128)(2,1)} async-done(((bf16[2,512,512]{2,1,0:T(8,128)(2,1)}), bf16[4,512,512]{2,1,0:T(8,128)(2,1)}) %all-gather.2.cloned.1.call-update) | async-done | bytes 2097168 | tf_op jit(solution)/shard_map/all_gather | solution.py:16
  44.7 2.5 %broadcast_in_dim.30 = f32[4,512,512]{2,1,0:T(8,128)} broadcast(f32[]{:T(128)} %constant.60.clone.1), dimensions={} | broadcast | bytes 4194308 | tf_op jit(solution)/shard_map/broadcast_in_dim | solution.py:39
  47.2 29.6 %while.17 = (s32[]{:T(128)}, f32[4,512,512]{2,1,0:T(8,128)}, pred[8]{0:T(512)(128)(4,1)S(1)}, s32[8]{0:T(128)S(1)}, bf16[8,512,512]{2,1,0:T(8,128)(2,1)}, /*inde...) while((s32[]{:T(128)}, f32[4,512,512]{2,1,0:T(8,128)}, ...), condition=%wide.region_3.4_spmd.clone, body=%wide.region_0.3_spmd.clone.sunk | while | flops 537657856 | bytes 3677518 | solution.py:52
  47.2 0.6 dynamic_slice.47
  48.5 9.7 %conditional.3 = (f32[4,512,512]{2,1,0:T(8,128)}) conditional(s32[]{:T(128)} %bitcast.25, f32[4,512,512]{2,1,0:T(8,128)} %get-tuple-element.314, (s32[]{:T(128)}, s32[8]{0:T(128)S(1)}, f32[4,512,512]{2,1,0:T(8,128)}, bf16[8,512,512]{2,1,0:T(8,128)(2,1)}, s32[8]{0:T(128)S(1)}, /*index=5*/s32[4]{0:T(128)S(1)}, s32[512]{0:T(512)S(1)}, ...), branch_computations={%region_1.0_spmd, %region_2.2_spmd} | conditional | flops 537657856 | bytes 3675286 | solution.py:50
  48.5 0.6 dynamic_slice.25
  51.0 0.6 dynamic_slice.26
  51.6 0.6 broadcast_compare_fusion
  52.2 0.6 dynamic_slice.22
  54.7 3.5 %fusion.3 = f32[4,512,512]{2,1,0:T(8,128)} fusion(f32[4,512,512]{2,1,0:T(8,128)} %get-tuple-element.188, s32[]{:T(128)S(6)} %select_n.37, bf16[8,512,512]{2,1,0:T(8,128)(2,1)} %get-tuple-element.196, s32[]{:T(128)S(6)} %select_n.36, bf16[4,512,512]{2,1,0:T(8,128)(2,1)} %get-tuple-element.195, s32[]{:T(128)S(6)} %select_n.38, ...), kind=kOutput, calls=%fused_computation.4 | convolution fusion | flops 537657344 | bytes 3672576 | tf_op jit(solution)/shard_map/while/body/eval_jaxpr/cond/branch_1_fun/dot_general | solution.py:32
  58.2 0.6 dynamic_slice.47
  59.4 9.7 %conditional.3 = (f32[4,512,512]{2,1,0:T(8,128)}) conditional(s32[]{:T(128)} %bitcast.25, f32[4,512,512]{2,1,0:T(8,128)} %get-tuple-element.314, (s32[]{:T(128)}, s32[8]{0:T(128)S(1)}, f32[4,512,512]{2,1,0:T(8,128)}, bf16[8,512,512]{2,1,0:T(8,128)(2,1)}, s32[8]{0:T(128)S(1)}, /*index=5*/s32[4]{0:T(128)S(1)}, s32[512]{0:T(512)S(1)}, ...), branch_computations={%region_1.0_spmd, %region_2.2_spmd} | conditional | flops 537657856 | bytes 3675286 | solution.py:50
  59.5 0.6 dynamic_slice.25
  61.9 0.6 dynamic_slice.26
  62.5 0.6 broadcast_compare_fusion
  63.2 0.6 dynamic_slice.22
  65.7 3.5 %fusion.3 = f32[4,512,512]{2,1,0:T(8,128)} fusion(f32[4,512,512]{2,1,0:T(8,128)} %get-tuple-element.188, s32[]{:T(128)S(6)} %select_n.37, bf16[8,512,512]{2,1,0:T(8,128)(2,1)} %get-tuple-element.196, s32[]{:T(128)S(6)} %select_n.36, bf16[4,512,512]{2,1,0:T(8,128)(2,1)} %get-tuple-element.195, s32[]{:T(128)S(6)} %select_n.38, ...), kind=kOutput, calls=%fused_computation.4 | convolution fusion | flops 537657344 | bytes 3672576 | tf_op jit(solution)/shard_map/while/body/eval_jaxpr/cond/branch_1_fun/dot_general | solution.py:32
  69.1 0.6 dynamic_slice.47
  70.4 0.6 dynamic_slice.47
  71.7 0.6 dynamic_slice.47
  73.0 0.6 dynamic_slice.47
  74.3 0.6 dynamic_slice.47
  75.5 0.6 dynamic_slice.47
  76.8 0.0 reduce-scatter.3.cloned.1.call-update
  76.8 0.0 reduce-scatter.5.cloned.1.call-start
  76.9 130.9 %reduce-scatter.3.cloned.1.call-done = f32[4,32,512]{2,1,0:T(8,128)} async-done(((f32[4,512,512]{2,1,0:T(8,128)}), f32[4,32,512]{2,1,0:T(8,128)}) %reduce-scatter.3.cloned.1.call-update) | async-done | bytes 262160 | tf_op jit(solution)/shard_map/reduce_scatter | solution.py:53
  207.8 0.6 gather_fusion
  208.5 0.1 broadcast_compare_fusion.1
  208.5 12.3 %reduce-scatter.5.cloned.1.call-done = f32[2,32,512]{2,1,0:T(8,128)} async-done(((f32[4,32,512]{2,1,0:T(8,128)}), f32[2,32,512]{2,1,0:T(8,128)}) %reduce-scatter.5.cloned.1.call-update) | async-done | bytes 131088 | tf_op jit(solution)/shard_map/reduce_scatter | solution.py:54
  220.8 1.6 broadcast_select_fusion
  (26 shorter events, 0.1 us)
Async XLA Ops:
  6.5 40.7 %copy-start = (s32[4]{0:T(128)S(1)}, s32[4]{0:T(128)}, u32[]{:S(2)}) copy-start(s32[4]{0:T(128)} %param.17) | copy-start | bytes 52
  6.5 40.7 %copy-start.2 = (s32[8]{0:T(128)S(1)}, s32[8]{0:T(128)}, u32[]{:S(2)}) copy-start(s32[8]{0:T(128)} %param.14) | copy-start | bytes 100
  6.5 40.7 %copy-start.1 = (s32[8]{0:T(128)S(1)}, s32[8]{0:T(128)}, u32[]{:S(2)}) copy-start(s32[8]{0:T(128)} %param.15) | copy-start | bytes 100
  6.5 38.2 %all-gather.2.cloned.1.call-start = ((), (), s32[]{:S(2)}) async-start(), calls=%async_computation.2 | async-start | bytes 3145728 | tf_op jit(solution)/shard_map/all_gather | solution.py:16
  7.3 200.5 %reduce-scatter.3.cloned.1.call-start = ((), (), s32[]{:S(2)}) async-start(), calls=%async_computation.3 | async-start | bytes 4456448 | tf_op jit(solution)/shard_map/reduce_scatter | solution.py:53
  76.8 144.0 %reduce-scatter.5.cloned.1.call-start = ((), (), s32[]{:S(2)}) async-start(), calls=%async_computation.4 | async-start | bytes 393216 | tf_op jit(solution)/shard_map/reduce_scatter | solution.py:54
Sparse Core Ops, SparseCore 0:
  8.9 35.8 all-gather.1
  76.9 130.7 reduce-scatter.2
  210.0 10.7 reduce-scatter.4
where the time goes:
time: 229 us
  waiting for transfers between devices  181 us (79%)
  between operations  13.8 us (6%)
  loops' own time  12.9 us (6%)
  local copies, waits for them, and re-layouts  11.6 us (5%)
  matrix products  6.96 us (3%)
  other arithmetic  2.99 us (1%)
    reduce_scatter x1, waiting for transfers between devices, local(): lax.psum_scatter(partial_value, 'term', scatter_dimension=1, tiled=True)  131 us
    all_gather x1, waiting for transfers between devices, local(): whole_wave = lax.all_gather(wavefunction, 'sector', axis=0, tiled=True)  36.8 us
    reduce_scatter x1, waiting for transfers between devices, local(): owned = lax.psum_scatter(shares, 'sector', scatter_dimension=0, tiled=True)  12.3 us
    another operation x8, loops' own time, apply_term(): lax.cond(live_mask[slot], contribute, lambda kept: kept, partial_value)  7.67 us
    dot_general x2, matrix products, term_product(): lax.dot_general(left_half, right_operators[slot], (((1,), (1,)), ((), ())...  6.96 us
    another operation x1, loops' own time, local(): partial_value = lax.fori_loop(0, slot_count, apply_term, partial_value)  5.24 us
    dynamic_slice x8, local copies, waits for them, and re-layouts, apply_term(): live_mask[slot]  4.82 us
  transfers between devices with their start and end apart: 3, of which 3 were waited for; matrix products, arithmetic and copies ran while one was open for 0% of the time, Pallas kernels for 0%

commit v1 on v0

v1 whole, which is shorter than its diff:
```python
import functools

import jax
import jax.numpy as jnp
from jax import lax
from jax.experimental import pallas as pl
from jax.experimental.pallas import tpu as pltpu
from jax.sharding import PartitionSpec as P

BF16 = jnp.bfloat16
F32 = jnp.float32


def kernel(
    dims,
    wave,
    left,
    right,
    source_ref,
    target_ref,
    live_ref,
    rows_ref,
    out,
    wv,
    lbuf,
    rbuf,
    prod,
    snd_a0,
    snd_b0,
    rcv_a0,
    rcv_b0,
    acc_a,
    acc_b,
    snd_a1,
    rcv_a1,
    snd_b1,
    rcv_b1,
    snd_a2,
    rcv_a2,
    snd_b2,
    rcv_b2,
    snd_a3,
    rcv_a3,
    snd_b3,
    rcv_b3,
    load_sem,
    g_send,
    g_recv,
    f_send,
    f_recv,
    s0,
    r0,
    sx,
    rx,
    sy_b,
    ry_b,
    sy_a,
    ry_a,
    sz_a,
    rz_a,
    sz_b,
    rz_b,
):
    Z, X, S, K, B, C = dims
    H = C // 2
    slots = left.shape[0]
    term = lax.axis_index("term")
    ym = lax.axis_index("sector")
    cm = lax.rem(term, 2)
    xm = lax.rem(term // 2, X)
    zm = term // (2 * X)
    co = 1 - cm
    xo = 1 - xm

    def dev(z, x, c, y):
        return ((z * X + x) * 2 + c, y)

    core_peer = dev(zm, xm, co, ym)
    x_peer = dev(zm, xo, cm, ym)

    def y_peer(d):
        return dev(zm, xm, cm, lax.rem(ym + d, S))

    def z_peer(d):
        return dev(lax.rem(zm + d, Z), xm, cm, ym)

    def remote(src, dst, ssem, rsem, peer):
        return pltpu.make_async_remote_copy(
            src_ref=src,
            dst_ref=dst,
            send_sem=ssem,
            recv_sem=rsem,
            device_id=peer,
            device_id_type=pl.DeviceIdType.MESH,
        )

    mine = pl.ds(ym * K, K)
    own_loads = []
    for n, half in enumerate((cm, co)):
        cols = pl.ds(pl.multiple_of(half * H, 128), H)
        own_loads.append(pltpu.make_async_copy(wave.at[:, :, cols], wv.at[half, mine], load_sem.at[n]))
    l_loads = [
        pltpu.make_async_copy(left.at[:, :, c], lbuf.at[c], load_sem.at[2 + c]) for c in range(2)
    ]
    r_load = pltpu.make_async_copy(right, rbuf, load_sem.at[4])
    for cp in own_loads:
        cp.start()
    for cp in l_loads:
        cp.start()
    r_load.start()

    barrier = pltpu.get_barrier_semaphore()
    peers = [core_peer, x_peer]
    peers += [y_peer(d) for d in range(1, S)]
    peers += [z_peer(d) for d in range(1, Z)]
    for peer in peers:
        pl.semaphore_signal(barrier, inc=1, device_id=peer, device_id_type=pl.DeviceIdType.MESH)
    pl.semaphore_wait(barrier, len(peers))

    own_loads[0].wait()
    gathers = []
    for d in range(1, S):
        cp = remote(wv.at[cm, mine], wv.at[cm, mine], g_send.at[d - 1], g_recv.at[d - 1], y_peer(d))
        cp.start()
        gathers.append(cp)
    own_loads[1].wait()
    forwards = []
    for d in range(1, S):
        theirs = pl.ds(lax.rem(ym + S - d, S) * K, K)
        remote(
            wv.at[cm, theirs], wv.at[cm, theirs], g_send.at[d - 1], g_recv.at[d - 1], y_peer(d)
        ).wait_recv()
        cp = remote(
            wv.at[cm, theirs], wv.at[cm, theirs], f_send.at[d - 1], f_recv.at[d - 1], core_peer
        )
        cp.start()
        forwards.append(cp)
    for cp in l_loads:
        cp.wait()
    r_load.wait()
    for d in range(1, S):
        theirs = pl.ds(lax.rem(ym + S - d, S) * K, K)
        remote(
            wv.at[co, theirs], wv.at[co, theirs], f_send.at[d - 1], f_recv.at[d - 1], core_peer
        ).wait_recv()

    depth_ids = lax.broadcasted_iota(jnp.int32, (1, wv.shape[2]), 1)

    def products(c):
        @pl.loop(0, slots)
        def _(t):
            source = source_ref[t]
            limit = jnp.where(t < live_ref[0], rows_ref[source], 0)
            keep = jnp.where(depth_ids < limit, 1.0, 0.0).astype(BF16)
            lmat = lbuf[c, t].reshape(Z * X * B, -1) * keep
            total = None
            for h in range(2):
                half = jnp.dot(lmat, wv[h, source], preferred_element_type=F32).astype(BF16)
                part = lax.dot_general(
                    half,
                    rbuf[t, :, h * H : (h + 1) * H],
                    (((1,), (1,)), ((), ())),
                    preferred_element_type=F32,
                )
                total = part if total is None else total + part
            prod[t] = total

    def sums(store):
        @pl.loop(0, S * K * Z * X)
        def _(n):
            s = n // (Z * X)
            zx = n % (Z * X)
            y, k = s // K, s % K
            z, x = zx // X, zx % X
            rows = pl.ds(pl.multiple_of(zx * B, B), B)
            total = jnp.zeros((B, C), F32)
            for t in range(slots):
                weight = jnp.where(target_ref[t] == s, 1.0, 0.0)
                total = total + prod[t, rows, :] * weight
            store(y, k, z, x, total)

    def store_send(y, k, z, x, total):
        snd_a0[x, y, z, k] = total[:, :H].astype(BF16)
        snd_b0[y, x, z, k] = total[:, H:].astype(BF16)

    def store_own(y, k, z, x, total):
        acc_a[x, y, z, k] = total[:, :H]
        acc_b[y, x, z, k] = total[:, H:]

    products(co)
    sums(store_send)
    a0 = remote(snd_a0, rcv_a0, s0.at[0], r0.at[0], core_peer)
    b0 = remote(snd_b0, rcv_b0, s0.at[1], r0.at[1], core_peer)
    a0.start()
    b0.start()
    products(cm)
    sums(store_own)

    a0.wait_recv()
    snd_a1[...] = (acc_a[xo] + rcv_a0[xo].astype(F32)).astype(BF16)
    a1 = remote(snd_a1, rcv_a1, sx.at[0], rx.at[0], x_peer)
    a1.start()
    b0.wait_recv()
    b1 = []
    for d in range(1, S):
        yo = lax.rem(ym + d, S)
        snd_b1[d - 1] = (acc_b[yo] + rcv_b0[yo].astype(F32)).astype(BF16)
        cp = remote(snd_b1.at[d - 1], rcv_b1.at[d - 1], sy_b.at[d - 1], ry_b.at[d - 1], y_peer(d))
        cp.start()
        b1.append(cp)

    a1.wait_recv()
    a2 = []
    for d in range(1, S):
        yo = lax.rem(ym + d, S)
        snd_a2[d - 1] = (
            acc_a[xm, yo] + rcv_a0[xm, yo].astype(F32) + rcv_a1[yo].astype(F32)
        ).astype(BF16)
        cp = remote(snd_a2.at[d - 1], rcv_a2.at[d - 1], sy_a.at[d - 1], ry_a.at[d - 1], y_peer(d))
        cp.start()
        a2.append(cp)
    for cp in b1:
        cp.wait_recv()

    def b_sum(x):
        total = acc_b[ym, x] + rcv_b0[ym, x].astype(F32)
        for d in range(1, S):
            total = total + rcv_b1[d - 1, x].astype(F32)
        return total

    snd_b2[...] = b_sum(xo).astype(BF16)
    b2 = remote(snd_b2, rcv_b2, sx.at[1], rx.at[1], x_peer)
    b2.start()

    def a_last(z):
        total = acc_a[xm, ym, z] + rcv_a0[xm, ym, z].astype(F32) + rcv_a1[ym, z].astype(F32)
        for d in range(1, S):
            total = total + rcv_a2[d - 1, z].astype(F32)
        return total

    def b_last(z):
        total = acc_b[ym, xm, z] + rcv_b0[ym, xm, z].astype(F32)
        for d in range(1, S):
            total = total + rcv_b1[d - 1, xm, z].astype(F32)
        return total + rcv_b2[z].astype(F32)

    for cp in a2:
        cp.wait_recv()
    a3, b3 = [], []
    for d in range(1, Z):
        snd_a3[d - 1] = a_last(lax.rem(zm + d, Z)).astype(BF16)
        cp = remote(snd_a3.at[d - 1], rcv_a3.at[d - 1], sz_a.at[d - 1], rz_a.at[d - 1], z_peer(d))
        cp.start()
        a3.append(cp)
    b2.wait_recv()
    for d in range(1, Z):
        snd_b3[d - 1] = b_last(lax.rem(zm + d, Z)).astype(BF16)
        cp = remote(snd_b3.at[d - 1], rcv_b3.at[d - 1], sz_b.at[d - 1], rz_b.at[d - 1], z_peer(d))
        cp.start()
        b3.append(cp)

    ids = term * B + lax.broadcasted_iota(jnp.int32, (B, H), 0)
    for own, copies, received, h in ((a_last, a3, rcv_a3, 0), (b_last, b3, rcv_b3, 1)):
        total = own(zm)
        for d, cp in enumerate(copies):
            cp.wait_recv()
            total = total + received[d].astype(F32)
        for k in range(K):
            used = ids < rows_ref[ym * K + k]
            out[k, :, h * H : (h + 1) * H] = jnp.where(used, total[k], 0.0)

    for cp in gathers + forwards + [a0, b0, a1, b2] + b1 + a2 + a3 + b3:
        cp.wait_send()


def local(mesh_sizes, wave, left, right, source, target, live, sector_rows):
    T, S = mesh_sizes
    X = 2
    Z = T // (2 * X)
    K, R, C = wave.shape
    B = R // T
    H = C // 2
    slots = left.shape[0]
    dims = (Z, X, S, K, B, C)
    left = left.reshape(slots, Z * X, 2, B, R)
    vm = pltpu.VMEM
    dma = pltpu.SemaphoreType.DMA
    full_a = (X, S, Z, K, B, H)
    full_b = (S, X, Z, K, B, H)
    scratch = [
        vm((2, S * K, R, H), BF16),
        vm((2, slots, Z * X, B, R), BF16),
        vm((slots, C, C), BF16),
        vm((slots, R // 2, C), F32),
        vm(full_a, BF16),
        vm(full_b, BF16),
        vm(full_a, BF16),
        vm(full_b, BF16),
        vm(full_a, F32),
        vm(full_b, F32),
        vm(full_a[1:], BF16),
        vm(full_a[1:], BF16),
        vm((S - 1,) + full_b[1:], BF16),
        vm((S - 1,) + full_b[1:], BF16),
        vm((S - 1, Z, K, B, H), BF16),
        vm((S - 1, Z, K, B, H), BF16),
        vm((Z, K, B, H), BF16),
        vm((Z, K, B, H), BF16),
        vm((Z - 1, K, B, H), BF16),
        vm((Z - 1, K, B, H), BF16),
        vm((Z - 1, K, B, H), BF16),
        vm((Z - 1, K, B, H), BF16),
        dma((5,)),
        dma((S - 1,)),
        dma((S - 1,)),
        dma((S - 1,)),
        dma((S - 1,)),
        dma((2,)),
        dma((2,)),
        dma((2,)),
        dma((2,)),
        dma((S - 1,)),
        dma((S - 1,)),
        dma((S - 1,)),
        dma((S - 1,)),
        dma((Z - 1,)),
        dma((Z - 1,)),
        dma((Z - 1,)),
        dma((Z - 1,)),
    ]
    any_spec = pl.BlockSpec(memory_space=pl.ANY)
    smem = pl.BlockSpec(memory_space=pltpu.SMEM)
    return pl.pallas_call(
        functools.partial(kernel, dims),
        out_shape=jax.ShapeDtypeStruct((K, B, C), F32),
        in_specs=[any_spec] * 3 + [smem] * 4,
        out_specs=pl.BlockSpec(memory_space=pltpu.VMEM),
        scratch_shapes=scratch,
        compiler_params=pltpu.CompilerParams(
            collective_id=0, has_side_effects=True, vmem_limit_bytes=60 * 1024 * 1024
        ),
    )(wave, left, right, source, target, live, sector_rows)


def solution(mesh):
    in_specs = (
        P("sector", None, None),
        P(("term", "sector"), None, None),
        P(("term", "sector"), None, None),
        P(("term", "sector")),
        P(("term", "sector")),
        P(("term", "sector")),
        P(),
    )
    out_specs = P("sector", "term", None)
    sizes = (mesh.shape["term"], mesh.shape["sector"])
    return jax.shard_map(
        functools.partial(local, sizes),
        mesh=mesh,
        in_specs=in_specs,
        out_specs=out_specs,
        check_vma=False,
    )
```

time: 229 us -> 54.3 us (0.24)
  waiting for transfers between devices: 181 us -> 0 us
  Pallas kernels: 0 us -> 51.9 us
  between operations: 13.8 us -> 0.66 us
  loops' own time: 12.9 us -> 0 us
  local copies, waits for them, and re-layouts: 11.6 us -> 1.57 us
  matrix products: 6.96 us -> 0 us
  other arithmetic: 2.99 us -> 0 us
    reduce_scatter x2 -> x0, waiting for transfers between devices: 143 us -> none  [the longest x1 131 us: local(): lax.psum_scatter(partial_value, 'term', scatter_dimension=1, tiled=True)]
    pallas_call x0 -> x1, Pallas kernels: none -> 51.9 us  [local(): pl.pallas_call(functools.partial(kernel, dims), out_shape=jax.ShapeDtypeS...]
    all_gather x1 -> x0, waiting for transfers between devices: 36.8 us -> none  [local(): whole_wave = lax.all_gather(wavefunction, 'sector', axis=0, tiled=True)]
    another operation x9 -> x0, loops' own time: 12.9 us -> none  [the longest x8 7.67 us: apply_term(): lax.cond(live_mask[slot], contribute, lambda kept: kept, partial_value)]
    dynamic_slice x14 -> x0, local copies, waits for them, and re-layouts: 8.43 us -> none  [the longest x8 4.82 us: apply_term(): live_mask[slot]]
    dot_general x2 -> x0, matrix products: 6.96 us -> none  [term_product(): lax.dot_general(left_half, right_operators[slot], (((1,), (1,)), ((), ())...]
    broadcast_in_dim x1 -> x0, local copies, waits for them, and re-layouts: 2.48 us -> none  [local(): partial_value = jnp.zeros((sector_count, row_count, col_count), jnp.float32)]
  transfers between devices with their start and end apart: 3 -> 0, of which waited for: 3 -> 0; matrix products, arithmetic and copies ran while one was open for 0% -> 0% of each run, Pallas kernels for 0% -> 0%
where the time goes in v1:
time: 54.3 us; the launch traced here: 54.2 us
  Pallas kernels  51.9 us (96%)
  local copies, waits for them, and re-layouts  1.57 us (3%)
  between operations  0.66 us (1%)
    pallas_call x1, Pallas kernels, local(): pl.pallas_call(functools.partial(kernel, dims), out_shape=jax.ShapeDtypeS...  51.9 us
    unnamed x1, local copies, waits for them, and re-layouts  1.57 us

profile of v1, /device:TPU:0, one launch (start us, length us, event | category | flops | bytes accessed | tf_op | source)
XLA Modules:
  0.0 54.2 jit_solution(1690673630753863977)
XLA Ops:
  0.7 51.9 %shard_map.73 = f32[2,32,512]{2,1,0:T(8,128)} custom-call(bf16[2,512,512]{2,1,0:T(8,128)(2,1)} %wave.1, bf16[8,8,2,32,512]{4,3,2,1,0:T(8,128)(2,1)} %bitcast.1, bf16[8,512,512]{2,1,0:T(8,128)(2,1)} %right.1, s32[8]{0:T(128)} %source_ref.1, s32[8]{0:T(128)} %target_ref.1, s32[1]{0:T(128)S(6)} %copy.9.live_ref, s32[4]{0:T(128)} %rows_ref.1), custom_call_target="tpu_custom_call" | custom-call | tf_op jit(solution)/shard_map/pallas_call | solution.py:333
  52.6 1.6 %copy.10 = f32[2,32,512]{2,1,0:T(8,128)} copy(f32[2,32,512]{2,1,0:T(8,128)} %shard_map.73) | data formatting | bytes 262144

commit v2 on v1

v2 whole, which is shorter than its diff:
```python
import functools

import jax
import jax.numpy as jnp
from jax import lax
from jax.experimental import pallas as pl
from jax.experimental.pallas import tpu as pltpu
from jax.sharding import PartitionSpec as P

BF16 = jnp.bfloat16
F32 = jnp.float32


def kernel(
    dims,
    wave,
    left,
    right,
    source_ref,
    target_ref,
    live_ref,
    rows_ref,
    out,
    near,
    far,
    lbuf,
    rbuf,
    prod,
    snd_a0,
    snd_b0,
    rcv_a0,
    rcv_b0,
    acc_a,
    acc_b,
    snd_a1,
    rcv_a1,
    snd_b1,
    rcv_b1,
    snd_a2,
    rcv_a2,
    snd_b2,
    rcv_b2,
    snd_a3,
    rcv_a3,
    snd_b3,
    rcv_b3,
    order,
    joins,
    load_sem,
    g_send,
    g_recv,
    h_send,
    h_recv,
    f_send,
    f_recv,
    s0,
    r0,
    sx,
    rx,
    sy_b,
    ry_b,
    sy_a,
    ry_a,
    sz,
    rz,
):
    Z, X, S, K, B, C = dims
    H, Q = C // 2, C // 4
    R = wave.shape[1]
    slots = left.shape[0]
    term = lax.axis_index("term")
    ym = lax.axis_index("sector")
    cm = lax.rem(term, 2)
    xm = lax.rem(term // 2, X)
    zm = term // (2 * X)
    co = 1 - cm
    xo = 1 - xm

    def dev(z, x, c, y):
        return ((z * X + x) * 2 + c, y)

    core_peer = dev(zm, xm, co, ym)
    x_peer = dev(zm, xo, cm, ym)

    def y_peer(d):
        return dev(zm, xm, cm, lax.rem(ym + d, S))

    def z_peer(d):
        return dev(lax.rem(zm + d, Z), xm, cm, ym)

    def remote(src, dst, ssem, rsem, peer):
        return pltpu.make_async_remote_copy(
            src_ref=src,
            dst_ref=dst,
            send_sem=ssem,
            recv_sem=rsem,
            device_id=peer,
            device_id_type=pl.DeviceIdType.MESH,
        )

    mine = pl.ds(ym * K, K)
    own_loads = []
    for n, (half, held) in enumerate(((xm, near), (xo, far))):
        cols = pl.ds(pl.multiple_of(half * H, 128), H)
        own_loads.append(
            pltpu.make_async_copy(wave.at[:, :, cols], held.at[mine], load_sem.at[n])
        )
    l_loads = [
        pltpu.make_async_copy(left.at[:, :, c], lbuf.at[:, c], load_sem.at[2 + c]) for c in range(2)
    ]
    l_loads += [
        pltpu.make_async_copy(right.at[:, :, h * H : (h + 1) * H], rbuf.at[h], load_sem.at[4 + h])
        for h in range(2)
    ]
    for cp in own_loads:
        cp.start()
    for cp in l_loads:
        cp.start()

    barrier = pltpu.get_barrier_semaphore()
    peers = [core_peer, x_peer]
    peers += [y_peer(d) for d in range(1, S)]
    peers += [z_peer(d) for d in range(1, Z)]
    for peer in peers:
        pl.semaphore_signal(barrier, inc=1, device_id=peer, device_id_type=pl.DeviceIdType.MESH)
    pl.semaphore_wait(barrier, len(peers))

    def part(held, d, j, c):
        sector = lax.rem(ym + S - d, S) * K + j // 4
        rows = pl.ds((j % 4) * (R // 4), R // 4)
        return held.at[sector, rows, pl.ds(pl.multiple_of(c * Q, 128), Q)]

    pieces = [(d, j) for j in range(4 * K) for d in range(1, S)]

    def y_copy(d, j, source):
        ref = part(near, source, j, cm)
        return remote(ref, ref, g_send.at[d - 1, j], g_recv.at[d - 1, j], y_peer(d))

    def x_copy(d, j):
        ref = part(near, d, j, cm)
        return remote(ref, part(far, d, j, cm), h_send.at[d - 1, j], h_recv.at[d - 1, j], x_peer)

    def core_copy(d, j, held, c, n):
        ref = part(held, d, j, c)
        return remote(ref, ref, f_send.at[n, d - 1, j], f_recv.at[n, d - 1, j], core_peer)

    sent = []
    own_loads[0].wait()
    for d, j in pieces:
        cp = y_copy(d, j, 0)
        cp.start()
        sent.append(cp)
    own_loads[1].wait()

    targets = [target_ref[t] for t in range(slots)]
    ranks = []
    for t in range(slots):
        rank = jnp.int32(0)
        for u in range(slots):
            ahead = targets[u] <= targets[t] if u < t else targets[u] < targets[t]
            if u != t:
                rank = rank + jnp.where(ahead, 1, 0)
        ranks.append(rank)
    before = jnp.int32(-1)
    for n in range(slots):
        slot, target = jnp.int32(0), jnp.int32(0)
        for t in range(slots):
            slot = jnp.where(ranks[t] == n, t, slot)
            target = jnp.where(ranks[t] == n, targets[t], target)
        order[n] = slot
        joins[n] = jnp.where(target == before, 1.0, 0.0)
        before = target
    prod[0] = jnp.zeros(prod.shape[1:], F32)
    for d, j in pieces:
        y_copy(d, j, d).wait_recv()
        for cp in (x_copy(d, j), core_copy(d, j, near, cm, 0)):
            cp.start()
            sent.append(cp)
    for cp in l_loads:
        cp.wait()
    for d, j in pieces:
        core_copy(d, j, near, co, 0).wait_recv()

    depth_ids = lax.broadcasted_iota(jnp.int32, (1, R), 1)
    chunk = 4 if slots % 8 == 0 else 1

    def products(held, h, first, begin, end):
        def one(n):
            t = order[n]
            source = source_ref[t]
            limit = jnp.where(t < live_ref[0], rows_ref[source], 0)
            keep = jnp.where(depth_ids < limit, 1.0, 0.0).astype(BF16)
            lmat = lbuf[t].reshape(R, R) * keep
            half = jnp.dot(lmat, held[source], preferred_element_type=F32).astype(BF16)
            return lax.dot_general(
                half,
                rbuf[h, t],
                (((1,), (1,)), ((), ())),
                preferred_element_type=F32,
            )

        @pl.loop(begin // chunk, end // chunk)
        def _(m):
            for u in range(chunk):
                n = m * chunk + u
                total = one(n)
                if not first:
                    total = total + prod[n + 1] + prod[n] * joins[n]
                prod[n + 1] = total

    def sums(c, store):
        @pl.loop(0, S * K * Z * X)
        def _(m):
            s = m // (Z * X)
            zx = m % (Z * X)
            y, k = s // K, s % K
            z, x = zx // X, zx % X
            rows = pl.ds(pl.multiple_of((c * Z * X + zx) * B, B), B)
            upto = jnp.int32(0)
            below = jnp.int32(0)
            for t in range(slots):
                upto = upto + jnp.where(target_ref[t] <= s, 1, 0)
                below = below + jnp.where(target_ref[t] < s, 1, 0)
            store(y, k, z, x, prod[upto, rows, :] * jnp.where(upto > below, 1.0, 0.0))

    def store_send(y, k, z, x, total):
        for i in range(2):
            snd_a0[i, x, y, z, k] = total[:, 2 * i * Q : (2 * i + 1) * Q].astype(BF16)
            snd_b0[i, y, x, z, k] = total[:, (2 * i + 1) * Q : (2 * i + 2) * Q].astype(BF16)

    def store_own(y, k, z, x, total):
        for i in range(2):
            acc_a[i, x, y, z, k] = total[:, 2 * i * Q : (2 * i + 1) * Q]
            acc_b[i, y, x, z, k] = total[:, (2 * i + 1) * Q : (2 * i + 2) * Q]

    products(near, xm, True, 0, slots // 2)
    for d, j in pieces:
        x_copy(d, j).wait_recv()
        cp = core_copy(d, j, far, cm, 1)
        cp.start()
        sent.append(cp)
    products(near, xm, True, slots // 2, slots)
    for d, j in pieces:
        core_copy(d, j, far, co, 1).wait_recv()
    products(far, xo, False, 0, slots)
    sums(co, store_send)
    a0, b0 = [], []
    for i in range(2):
        a0.append(remote(snd_a0.at[i], rcv_a0.at[i], s0.at[0, i], r0.at[0, i], core_peer))
        b0.append(remote(snd_b0.at[i], rcv_b0.at[i], s0.at[1, i], r0.at[1, i], core_peer))
        a0[i].start()
        b0[i].start()
    sums(cm, store_own)

    a1, b1 = [], [[], []]
    for i in range(2):
        a0[i].wait_recv()
        snd_a1[i] = (acc_a[i, xo] + rcv_a0[i, xo].astype(F32)).astype(BF16)
        cp = remote(snd_a1.at[i], rcv_a1.at[i], sx.at[0, i], rx.at[0, i], x_peer)
        cp.start()
        a1.append(cp)
        b0[i].wait_recv()
        for d in range(1, S):
            yo = lax.rem(ym + d, S)
            snd_b1[i, d - 1] = (acc_b[i, yo] + rcv_b0[i, yo].astype(F32)).astype(BF16)
            cp = remote(
                snd_b1.at[i, d - 1],
                rcv_b1.at[i, d - 1],
                sy_b.at[i, d - 1],
                ry_b.at[i, d - 1],
                y_peer(d),
            )
            cp.start()
            b1[i].append(cp)

    def b_sum(i, x):
        total = acc_b[i, ym, x] + rcv_b0[i, ym, x].astype(F32)
        for d in range(1, S):
            total = total + rcv_b1[i, d - 1, x].astype(F32)
        return total

    a2, b2 = [[], []], []
    for i in range(2):
        a1[i].wait_recv()
        for d in range(1, S):
            yo = lax.rem(ym + d, S)
            snd_a2[i, d - 1] = (
                acc_a[i, xm, yo] + rcv_a0[i, xm, yo].astype(F32) + rcv_a1[i, yo].astype(F32)
            ).astype(BF16)
            cp = remote(
                snd_a2.at[i, d - 1],
                rcv_a2.at[i, d - 1],
                sy_a.at[i, d - 1],
                ry_a.at[i, d - 1],
                y_peer(d),
            )
            cp.start()
            a2[i].append(cp)
        for cp in b1[i]:
            cp.wait_recv()
        snd_b2[i] = b_sum(i, xo).astype(BF16)
        cp = remote(snd_b2.at[i], rcv_b2.at[i], sx.at[1, i], rx.at[1, i], x_peer)
        cp.start()
        b2.append(cp)

    def a_last(i, z):
        total = (
            acc_a[i, xm, ym, z]
            + rcv_a0[i, xm, ym, z].astype(F32)
            + rcv_a1[i, ym, z].astype(F32)
        )
        for d in range(1, S):
            total = total + rcv_a2[i, d - 1, z].astype(F32)
        return total

    def b_last(i, z):
        total = acc_b[i, ym, xm, z] + rcv_b0[i, ym, xm, z].astype(F32)
        for d in range(1, S):
            total = total + rcv_b1[i, d - 1, xm, z].astype(F32)
        return total + rcv_b2[i, z].astype(F32)

    z3 = []
    far_first = sorted(range(1, Z), key=lambda d: -min(d, Z - d))
    for i in range(2):
        for cp in a2[i]:
            cp.wait_recv()
        for n, own, snd, rcv in ((0, a_last, snd_a3, rcv_a3), (1, b_last, snd_b3, rcv_b3)):
            if n == 1:
                b2[i].wait_recv()
            copies = {}
            for d in far_first:
                snd[i, d - 1] = own(i, lax.rem(zm + d, Z)).astype(BF16)
                cp = remote(
                    snd.at[i, d - 1],
                    rcv.at[i, d - 1],
                    sz.at[n, i, d - 1],
                    rz.at[n, i, d - 1],
                    z_peer(d),
                )
                cp.start()
                copies[d] = cp
            z3.append((i, n, own, rcv, copies))

    ids = term * B + lax.broadcasted_iota(jnp.int32, (B, Q), 0)
    for i, n, own, rcv, copies in z3:
        total = own(i, zm)
        for d in range(1, Z):
            copies[d].wait_recv()
            total = total + rcv[i, d - 1].astype(F32)
            sent.append(copies[d])
        col = (2 * i + n) * Q
        for k in range(K):
            used = ids < rows_ref[ym * K + k]
            out[k, :, col : col + Q] = jnp.where(used, total[k], 0.0)

    sent += a0 + b0 + a1 + b2 + b1[0] + b1[1] + a2[0] + a2[1]
    for cp in sent:
        cp.wait_send()


def local(mesh_sizes, wave, left, right, source, target, live, sector_rows):
    T, S = mesh_sizes
    X = 2
    Z = T // (2 * X)
    K, R, C = wave.shape
    B = R // T
    H, Q = C // 2, C // 4
    slots = left.shape[0]
    dims = (Z, X, S, K, B, C)
    left = left.reshape(slots, Z * X, 2, B, R)
    vm = pltpu.VMEM
    dma = pltpu.SemaphoreType.DMA
    full_a = (2, X, S, Z, K, B, Q)
    full_b = (2, S, X, Z, K, B, Q)
    after_x = (2, S, Z, K, B, Q)
    after_y = (2, S - 1, X, Z, K, B, Q)
    both = (2, Z, K, B, Q)
    after_y2 = (2, S - 1, Z, K, B, Q)
    last = (2, Z - 1, K, B, Q)
    scratch = [
        vm((S * K, R, H), BF16),
        vm((S * K, R, H), BF16),
        vm((slots, 2, Z * X, B, R), BF16),
        vm((2, slots, C, H), BF16),
        vm((slots + 1, R, C), F32),
        vm(full_a, BF16),
        vm(full_b, BF16),
        vm(full_a, BF16),
        vm(full_b, BF16),
        vm(full_a, F32),
        vm(full_b, F32),
        vm(after_x, BF16),
        vm(after_x, BF16),
        vm(after_y, BF16),
        vm(after_y, BF16),
        vm(after_y2, BF16),
        vm(after_y2, BF16),
        vm(both, BF16),
        vm(both, BF16),
        vm(last, BF16),
        vm(last, BF16),
        vm(last, BF16),
        vm(last, BF16),
        pltpu.SMEM((slots,), jnp.int32),
        pltpu.SMEM((slots,), F32),
        dma((6,)),
        dma((S - 1, 4 * K)),
        dma((S - 1, 4 * K)),
        dma((S - 1, 4 * K)),
        dma((S - 1, 4 * K)),
        dma((2, S - 1, 4 * K)),
        dma((2, S - 1, 4 * K)),
        dma((2, 2)),
        dma((2, 2)),
        dma((2, 2)),
        dma((2, 2)),
        dma((2, S - 1)),
        dma((2, S - 1)),
        dma((2, S - 1)),
        dma((2, S - 1)),
        dma((2, 2, Z - 1)),
        dma((2, 2, Z - 1)),
    ]
    any_spec = pl.BlockSpec(memory_space=pl.ANY)
    smem = pl.BlockSpec(memory_space=pltpu.SMEM)
    return pl.pallas_call(
        functools.partial(kernel, dims),
        out_shape=jax.ShapeDtypeStruct((K, B, C), F32),
        in_specs=[any_spec] * 3 + [smem] * 4,
        out_specs=pl.BlockSpec(memory_space=pltpu.VMEM),
        scratch_shapes=scratch,
        compiler_params=pltpu.CompilerParams(
            collective_id=0, has_side_effects=True, vmem_limit_bytes=60 * 1024 * 1024
        ),
    )(wave, left, right, source, target, live, sector_rows)


def solution(mesh):
    in_specs = (
        P("sector", None, None),
        P(("term", "sector"), None, None),
        P(("term", "sector"), None, None),
        P(("term", "sector")),
        P(("term", "sector")),
        P(("term", "sector")),
        P(),
    )
    out_specs = P("sector", "term", None)
    sizes = (mesh.shape["term"], mesh.shape["sector"])
    return jax.shard_map(
        functools.partial(local, sizes),
        mesh=mesh,
        in_specs=in_specs,
        out_specs=out_specs,
        check_vma=False,
    )
```

time: 54.3 us -> 44 us (0.81)
  Pallas kernels: 51.9 us -> 41.6 us
    pallas_call x1, Pallas kernels: 51.9 us -> 41.6 us  [local(): pl.pallas_call(functools.partial(kernel, dims), out_shape=jax.ShapeDtypeS...]
where the time goes in v2:
time: 44 us; the launch traced here: 43.9 us
  Pallas kernels  41.6 us (95%)
  local copies, waits for them, and re-layouts  1.57 us (4%)
  between operations  0.66 us (2%)
    pallas_call x1, Pallas kernels, local(): pl.pallas_call(functools.partial(kernel, dims), out_shape=jax.ShapeDtypeS...  41.6 us
    unnamed x1, local copies, waits for them, and re-layouts  1.57 us

profile of v2, /device:TPU:0, one launch (start us, length us, event | category | flops | bytes accessed | tf_op | source)
XLA Modules:
  0.0 43.9 jit_solution(8406140283481207721)
XLA Ops:
  0.7 41.6 %shard_map.73 = f32[2,32,512]{2,1,0:T(8,128)} custom-call(bf16[2,512,512]{2,1,0:T(8,128)(2,1)} %wave.1, bf16[8,8,2,32,512]{4,3,2,1,0:T(8,128)(2,1)} %bitcast.1, bf16[8,512,512]{2,1,0:T(8,128)(2,1)} %right.1, s32[8]{0:T(128)} %source_ref.1, s32[8]{0:T(128)} %target_ref.1, s32[1]{0:T(128)S(6)} %copy.9.live_ref, s32[4]{0:T(128)} %rows_ref.1), custom_call_target="tpu_custom_call" | custom-call | tf_op jit(solution)/shard_map/pallas_call | solution.py:426
  42.3 1.6 %copy.10 = f32[2,32,512]{2,1,0:T(8,128)} copy(f32[2,32,512]{2,1,0:T(8,128)} %shard_map.73) | data formatting | bytes 262144
